TPU v7x, 32 devices: a whole 2x2x4 slice. The times are simulated.
32 devices in a mesh: grp: 8 (over z, y), row: 4 (over x, core).
Axes of the slice: x: 2, y: 2, z: 4, core: 2. Of those that a mesh axis runs over, the one named last changes fastest.
Arguments:
- block: bfloat16 [8192, 1024], P(('grp', 'row')), may hold values from -6 to 6
- degree: int32 [8192], P(('grp', 'row')), may hold values from 1 to 3
- tile_values: bfloat16 [2048, 128, 128], P(('grp', 'row')), may hold values from -0.1875 to 0.1875
- tile_rows: int32 [2048], P(('grp', 'row')), may hold values from 0 to 1
- tile_cols: int32 [2048], P(('grp', 'row')), may hold values from 0 to 15
- tile_count: int32 [32], P(('grp', 'row')), may hold values from 24 to 64, as said below
- send_tiles: int32 [32, 8], P(('grp', 'row')), may hold values from 0 to 1
Outputs:
- logs: bfloat16 [8192, 1024], P(('grp', 'row'))
- gram: float32 [8192, 1024], P(('grp', 'row'))
Inputs may be any that keep to these rules, and one draw needn't show every extreme that they name: Slots of a device at positions tile_count or later are padding; some device has all 64 slots live.
All inputs are finite; a program needn't handle non-finite values.
Results may differ from a plain program's by a relative error of at most 0.014.
Values may be sent and summed in bfloat16 or wider, within the bound.
A program may use at most 128 MiB of HBM per device.

v0:
```python
import functools

import jax
import jax.numpy as jnp
from jax import lax
from jax.experimental import pallas as pl
from jax.experimental.pallas import tpu as pltpu
from jax.sharding import PartitionSpec as P

POWERS = 2
MESH = pl.DeviceIdType.MESH


def order_kernel(sources, rows_ref, cols_ref, count_ref, before_ref, last_ref):
    slots = rows_ref.shape[0]

    def clear(place, carry):
        last_ref[place] = slots
        return carry

    def skip(slot, carry):
        before_ref[slot] = slots
        return carry

    def link(slot, carry):
        place = rows_ref[slot] * sources + cols_ref[slot]
        before_ref[slot] = last_ref[place]
        last_ref[place] = slot
        return carry

    lax.fori_loop(0, last_ref.shape[0], clear, 0)
    lax.fori_loop(0, slots, skip, 0)
    lax.fori_loop(0, count_ref[0], link, 0)


def step_kernel(
    groups, ranks, send_ref, before_ref, last_ref, degree_ref, values_hbm, block_ref, logs_ref, gram_ref,
    values_ref, sums, matrix_ref, values_sem, source, own, staged, total, everyone, mine,
    grp_send, grp_recv, row_send, row_recv, pass_send,
):
    chunks, _, row_tiles, tile, width = own.shape
    local = ranks * row_tiles
    g = lax.axis_index("grp")
    r = lax.axis_index("row")
    core = lax.rem(r, 2)
    partner = r + 1 - 2 * core
    pairs = ranks // 2

    slots = values_ref.shape[0]
    sources = source.shape[2]
    load = pltpu.make_async_copy(values_hbm, values_ref, values_sem)
    load.start()

    def other_group(step):
        return lax.rem(g + step, groups)

    def same_core(step):
        return lax.rem(r + 2 * step, ranks)

    barrier = pltpu.get_barrier_semaphore()
    for step in range(1, groups):
        pl.semaphore_signal(barrier, inc=1, device_id=(other_group(step), r), device_id_type=MESH)
    for step in range(1, ranks):
        pl.semaphore_signal(barrier, inc=1, device_id=(g, lax.rem(r + step, ranks)), device_id_type=MESH)

    def land(phase, j, rank):
        where = pl.ds(rank * row_tiles, row_tiles)
        return source.at[phase, j, where] if phase < POWERS else everyone.at[j, where]

    def row_copy(phase, j, to):
        origin = own.at[j, phase]
        return pltpu.make_async_remote_copy(
            src_ref=origin, dst_ref=land(phase, j, r),
            send_sem=row_send.at[phase, j, to], recv_sem=row_recv.at[phase, j, r],
            device_id=(g, to), device_id_type=MESH)

    def pass_copy(phase, j, rank):
        spot = land(phase, j, rank)
        return pltpu.make_async_remote_copy(
            src_ref=spot, dst_ref=spot,
            send_sem=pass_send.at[phase, j, rank], recv_sem=row_recv.at[phase, j, rank],
            device_id=(g, partner), device_id_type=MESH)

    def row_arrival(phase, j, rank):
        spot = land(phase, j, rank)
        return pltpu.make_async_remote_copy(
            src_ref=spot, dst_ref=spot,
            send_sem=pass_send.at[phase, j, rank], recv_sem=row_recv.at[phase, j, rank],
            device_id=(g, partner), device_id_type=MESH)

    def grp_copy(phase, j, to):
        return pltpu.make_async_remote_copy(
            src_ref=staged.at[phase, j, to], dst_ref=source.at[phase, j, local + g],
            send_sem=grp_send.at[phase, j, to], recv_sem=grp_recv.at[phase, j, g],
            device_id=(to, r), device_id_type=MESH)

    def grp_arrival(phase, j, group):
        return pltpu.make_async_remote_copy(
            src_ref=staged.at[phase, j, group], dst_ref=source.at[phase, j, local + group],
            send_sem=grp_send.at[phase, j, group], recv_sem=grp_recv.at[phase, j, group],
            device_id=(group, r), device_id_type=MESH)

    def stage(phase, j):
        for step in range(1, groups):
            to = other_group(step)
            staged[phase, j, to] = own[j, phase, send_ref[0, to]]
        source[phase, j, local + g] = own[j, phase, send_ref[0, g]]

    def keep(phase, j, value):
        tiles = value.reshape(row_tiles, tile, width)
        own[j, phase] = tiles
        if phase < POWERS:
            source[phase, j, pl.ds(r * row_tiles, row_tiles)] = tiles
        else:
            everyone[j, pl.ds(r * row_tiles, row_tiles)] = tiles

    def send(phase, j):
        if phase < POWERS:
            for step in sorted(range(1, groups), key=lambda step: abs(2 * step - groups)):
                grp_copy(phase, j, other_group(step)).start()
        for step in range(1, pairs):
            row_copy(phase, j, same_core(step)).start()
        row_copy(phase, j, partner).start()

    def receive(phase, j):
        for step in range(1, pairs):
            rank = lax.rem(r + ranks - 2 * step, ranks)
            row_arrival(phase, j, rank).wait_recv()
            pass_copy(phase, j, rank).start()
        row_arrival(phase, j, partner).wait_recv()
        for step in range(1, pairs):
            row_arrival(phase, j, lax.rem(partner + ranks - 2 * step, ranks)).wait_recv()
        if phase < POWERS:
            for step in range(1, groups):
                grp_arrival(phase, j, lax.rem(g + groups - step, groups)).wait_recv()

    for j in range(chunks):
        keep(0, j, block_ref[:, j * width : (j + 1) * width])
        stage(0, j)
    pl.semaphore_wait(barrier, groups + ranks - 2)
    for j in range(chunks):
        send(0, j)
    def clear(slot, carry):
        sums[slot] = jnp.zeros(sums.shape[1:], jnp.float32)
        return carry

    def add_slot(slot, carry):
        sums[slot] = sums[before_ref[slot]] + values_ref[slot].astype(jnp.float32)
        return carry

    lax.fori_loop(0, slots + 1, clear, 0)
    load.wait()
    lax.fori_loop(0, slots, add_slot, 0)
    for row in range(row_tiles):
        degree = degree_ref[row : row + 1, :].astype(jnp.float32)
        scale = (1.0 / jnp.broadcast_to(degree, (tile, tile))).T
        for col in range(sources):
            part = sums[last_ref[row * sources + col]] * scale
            matrix_ref[row * tile : (row + 1) * tile, col * tile : (col + 1) * tile] = part.astype(jnp.bfloat16)
    for phase in range(POWERS):
        for j in range(chunks):
            receive(phase, j)
            summed = jnp.dot(
                matrix_ref[...], source[phase, j].reshape(-1, width),
                preferred_element_type=jnp.float32)
            current = summed.astype(jnp.bfloat16)
            if phase == 0:
                total[j] = current.astype(jnp.float32)
            else:
                total[j] += current.astype(jnp.float32)
            if phase < POWERS - 1:
                keep(phase + 1, j, current)
                stage(phase + 1, j)
            else:
                logs = jnp.log(jnp.maximum(3.0 * total[j], 1.0)).astype(jnp.bfloat16)
                logs_ref[:, j * width : (j + 1) * width] = logs
                keep(phase + 1, j, logs)
            send(phase + 1, j)
    for j in range(chunks):
        receive(POWERS, j)
    mine[...] = everyone[r].reshape(-1, width).T
    rows_all = row_tiles * tile * ranks
    for j in range(chunks):
        part = jnp.dot(mine[...], everyone[j].reshape(-1, width), preferred_element_type=jnp.float32)
        gram_ref[:, j * width : (j + 1) * width] = part / rows_all
    for phase in range(POWERS + 1):
        for j in range(chunks):
            if phase < POWERS:
                for step in range(1, groups):
                    grp_copy(phase, j, other_group(step)).wait_send()
            for step in range(1, pairs):
                row_copy(phase, j, same_core(step)).wait_send()
                pass_copy(phase, j, lax.rem(r + ranks - 2 * step, ranks)).wait_send()
            row_copy(phase, j, partner).wait_send()


def body(block, degree, tile_values, tile_rows, tile_cols, tile_count, send_tiles):
    rows_here, width = block.shape
    tile = tile_values.shape[1]
    row_tiles = rows_here // tile
    ranks = lax.axis_size("row")
    groups = lax.axis_size("grp")
    sources = ranks * row_tiles + groups
    smem = pl.BlockSpec(memory_space=pltpu.SMEM)
    vmem = pl.BlockSpec(memory_space=pltpu.VMEM)
    slots = tile_values.shape[0]
    before, last = pl.pallas_call(
        functools.partial(order_kernel, sources),
        out_shape=(
            jax.ShapeDtypeStruct((slots,), jnp.int32),
            jax.ShapeDtypeStruct((row_tiles * sources,), jnp.int32),
        ),
        in_specs=[smem, smem, smem],
        out_specs=(smem, smem),
        name="order",
    )(tile_rows, tile_cols, tile_count)
    share = width // ranks
    chunks = ranks
    dma = pltpu.SemaphoreType.DMA
    logs, gram = pl.pallas_call(
        functools.partial(step_kernel, groups, ranks),
        out_shape=(
            jax.ShapeDtypeStruct((rows_here, width), jnp.bfloat16),
            jax.ShapeDtypeStruct((share, width), jnp.float32),
        ),
        in_specs=[smem, smem, smem, vmem, pl.BlockSpec(memory_space=pl.ANY), vmem],
        out_specs=(vmem, vmem),
        scratch_shapes=[
            pltpu.VMEM(tile_values.shape, jnp.bfloat16),
            pltpu.VMEM((slots + 1, tile, tile), jnp.float32),
            pltpu.VMEM((rows_here, sources * tile), jnp.bfloat16),
            dma,
            pltpu.VMEM((POWERS, chunks, sources, tile, share), jnp.bfloat16),
            pltpu.VMEM((chunks, POWERS + 1, row_tiles, tile, share), jnp.bfloat16),
            pltpu.VMEM((POWERS, chunks, groups, tile, share), jnp.bfloat16),
            pltpu.VMEM((chunks, rows_here, share), jnp.float32),
            pltpu.VMEM((chunks, ranks * row_tiles, tile, share), jnp.bfloat16),
            pltpu.VMEM((share, rows_here * ranks), jnp.bfloat16),
            dma((POWERS, chunks, groups)),
            dma((POWERS, chunks, groups)),
            dma((POWERS + 1, chunks, ranks)),
            dma((POWERS + 1, chunks, ranks)),
            dma((POWERS + 1, chunks, ranks)),
        ],
        compiler_params=pltpu.CompilerParams(
            collective_id=0, has_side_effects=True, vmem_limit_bytes=60 * 1024 * 1024),
        name="step",
    )(send_tiles, before, last, degree.reshape(row_tiles, tile), tile_values, block)
    return logs, gram


def solution(mesh):
    placed = (
        P(("grp", "row"), None),
        P(("grp", "row")),
        P(("grp", "row"), None, None),
        P(("grp", "row")),
        P(("grp", "row")),
        P(("grp", "row")),
        P(("grp", "row"), None),
    )
    return jax.shard_map(
        body,
        mesh=mesh,
        in_specs=placed,
        out_specs=(P(("grp", "row"), None), P(("grp", "row"), None)),
        check_vma=False,
    )
```

profile of v0, /device:TPU:1, one launch (start us, length us, event | category | flops | bytes accessed | tf_op | source)
XLA Modules:
  0.0 114.2 jit_solution(12926513782095206072)
XLA Ops:
  1.3 2.2 %order.1 = (s32[64]{0:T(128)}, s32[32]{0:T(128)}) custom-call(s32[64]{0:T(128)} %rows_ref.1, s32[64]{0:T(128)} %cols_ref.1, s32[1]{0:T(128)S(6)} %copy.11.count_ref), custom_call_target="tpu_custom_call" | custom-call | tf_op jit(solution)/shard_map/order/pallas_call | solution.py:207
  3.5 106.5 %step.1 = (bf16[256,1024]{1,0:T(8,128)(2,1)}, f32[256,1024]{1,0:T(8,128)}) custom-call(s32[1,8]{1,0:T(1,128)} %send_ref.1, s32[64]{0:T(128)} %get-tuple-element.4.before_ref, s32[32]{0:T(128)} %get-tuple-element.5.last_ref, s32[2,128]{1,0:T(2,128)} %bitcast.1, bf16[64,128,128]{2,1,0:T(8,128)(2,1)} %values_hbm.1, bf16[256,1024]{1,0:T(8,128)(2,1)} %block_ref.1), custom_call_target="tpu_custom_call" | custom-call | tf_op jit(solution)/shard_map/step/pallas_call | solution.py:220
  110.0 1.9 %copy.12 = bf16[256,1024]{1,0:T(8,128)(2,1)} copy(bf16[256,1024]{1,0:T(8,128)(2,1)} %get-tuple-element.8) | data formatting | bytes 1048576
  111.9 2.3 %copy.13 = f32[256,1024]{1,0:T(8,128)} copy(f32[256,1024]{1,0:T(8,128)} %get-tuple-element.9) | data formatting | bytes 2097152
where the time goes:
time: 115 us; the launch traced here: 114 us
  Pallas kernels  109 us (95%)
  local copies, waits for them, and re-layouts  4.17 us (4%)
  between operations  1.29 us (1%)
    pallas_call x1, Pallas kernels, body(): pl.pallas_call(functools.partial(step_kernel, groups, ranks), out_shape=(...  106 us
    unnamed x2, local copies, waits for them, and re-layouts  4.17 us

commit v1 on v0

v1 whole, which is shorter than its diff:
```python
import functools

import jax
import jax.numpy as jnp
from jax import lax
from jax.experimental import pallas as pl
from jax.experimental.pallas import tpu as pltpu
from jax.sharding import PartitionSpec as P

POWERS = 2
LINE = 4
CHUNKS = 8
AHEAD = 2
LAG_JOIN = 2
LAG_FINISH = 2
LAG_RELAY = 4
LAG_PASS = 4
MESH = pl.DeviceIdType.MESH


def relays_after(n, first, chunks, steps):
    near = [n + 2] if n + 2 < chunks else []
    later = [m for m in (n + LAG_RELAY,) if chunks <= m < steps]
    if n == first:
        later = [m for m in range(chunks, n + LAG_RELAY) if m < steps] + later
    return near + later


def order_kernel(sources, rows_ref, cols_ref, count_ref, before_ref, last_ref):
    slots = rows_ref.shape[0]

    def clear(place, carry):
        last_ref[place] = slots
        return carry

    def skip(slot, carry):
        before_ref[slot] = slots
        return carry

    def link(slot, carry):
        place = rows_ref[slot] * sources + cols_ref[slot]
        before_ref[slot] = last_ref[place]
        last_ref[place] = slot
        return carry

    lax.fori_loop(0, last_ref.shape[0], clear, 0)
    lax.fori_loop(0, slots, skip, 0)
    lax.fori_loop(0, count_ref[0], link, 0)


def step_kernel(
    groups, ranks, send_ref, before_ref, last_ref, degree_ref, values_hbm, block_ref, logs_ref, gram_ref,
    values_ref, values_sem, sums, near, across, table, given, spread,
    source, line, outgoing, incoming, joint, held, mixed, total, everyone, mine,
    row_send, row_recv, pass_send, up_send, relay_send, line_recv, part_send, part_recv, joint_recv,
    give_send, give_recv, table_send, table_recv,
):
    _, chunks, local, tile, width = source.shape
    row_tiles = line.shape[3]
    rows_here = row_tiles * tile
    lanes = groups // LINE
    g = lax.axis_index("grp")
    r = lax.axis_index("row")
    z = g // lanes
    y = lax.rem(g, lanes)
    half = z // 2
    inner = lax.rem(z + half, 2)
    hub = 1 + half
    far = 2 - half
    end = 3 * half
    far_end = 3 - 3 * half
    onward = hub + inner * (far - hub)
    core = lax.rem(r, 2)
    partner = r + 1 - 2 * core
    pairs = ranks // 2

    slots = values_ref.shape[0]
    load = pltpu.make_async_copy(values_hbm, values_ref, values_sem)
    load.start()

    def at(place, lane):
        return (place * lanes + lane, r)

    def lane_after(step):
        return lax.rem(y + step, lanes)

    def lane_before(step):
        return lax.rem(y + lanes - step, lanes)

    def same_core(step):
        return lax.rem(r + 2 * step, ranks)

    barrier = pltpu.get_barrier_semaphore()
    for step in range(1, groups):
        pl.semaphore_signal(barrier, inc=1, device_id=(lax.rem(g + step, groups), r), device_id_type=MESH)
    for step in range(1, ranks):
        pl.semaphore_signal(barrier, inc=1, device_id=(g, lax.rem(r + step, ranks)), device_id_type=MESH)

    def remote(src, dst, send_sem, recv_sem, to):
        return pltpu.make_async_remote_copy(
            src_ref=src, dst_ref=dst, send_sem=send_sem, recv_sem=recv_sem, device_id=to, device_id_type=MESH)

    def land(phase, j, rank):
        where = pl.ds(rank * row_tiles, row_tiles)
        return source.at[phase, j, where] if phase < POWERS else everyone.at[j, where]

    def row_copy(phase, j, to):
        spot = land(phase, j, r)
        return remote(spot, spot, row_send.at[phase, j, to], row_recv.at[phase, j, r], (g, to))

    def pass_copy(phase, j, rank):
        spot = land(phase, j, rank)
        return remote(spot, spot, pass_send.at[phase, j, rank], row_recv.at[phase, j, rank], (g, partner))

    def up_copy(phase, j):
        return remote(
            land(phase, j, r), line.at[phase, j, z], up_send.at[phase, j], line_recv.at[phase, j, z],
            at(onward, y))

    def relay_copy(phase, j):
        spot = line.at[phase, j, end]
        return remote(spot, spot, relay_send.at[phase, j], line_recv.at[phase, j, end], at(far, y))

    def line_arrival(phase, j, place):
        spot = line.at[phase, j, place]
        return remote(spot, spot, relay_send.at[phase, j], line_recv.at[phase, j, place], at(far, y))

    def joined(j):
        return j % 2 == 0

    def part_copy(phase, j, side, step):
        if side and step and joined(j):
            return remote(
                outgoing.at[j, side, step], joint.at[phase, j // 2, step],
                part_send.at[phase, j, side, step], joint_recv.at[phase, j // 2, step],
                at(hub, lane_after(step)))
        return remote(
            outgoing.at[j, side, step], incoming.at[phase, j, step],
            part_send.at[phase, j, side, step], part_recv.at[phase, j, step],
            at(end if side else hub, lane_after(step)))

    def give_copy(side, step):
        return remote(
            across.at[lane_before(step)], given.at[side, step],
            give_send.at[step], give_recv.at[side, step], at(hub, lane_before(step)))

    def table_copy(to):
        return remote(table.at[z], table.at[z], table_send.at[to], table_recv.at[z], at(to, y))

    def table_arrival(place):
        return remote(table.at[place], table.at[place], table_send.at[place], table_recv.at[place], at(far, y))

    def keep(phase, j, value):
        tiles = value.reshape(row_tiles, tile, width)
        if phase < POWERS:
            source[phase, j, pl.ds(r * row_tiles, row_tiles)] = tiles
            line[phase, j, z] = tiles
        else:
            everyone[j, pl.ds(r * row_tiles, row_tiles)] = tiles

    def row_start(phase, j):
        for step in range(1, pairs):
            row_copy(phase, j, same_core(step)).start()
        row_copy(phase, j, partner).start()

    def row_pass(phase, j):
        for step in range(1, pairs):
            rank = lax.rem(r + ranks - 2 * step, ranks)
            pass_copy(phase, j, rank).wait_recv()
            pass_copy(phase, j, rank).start()

    def row_wait(phase, j):
        pass_copy(phase, j, partner).wait_recv()
        for step in range(1, pairs):
            pass_copy(phase, j, lax.rem(partner + ranks - 2 * step, ranks)).wait_recv()

    for group in range(groups):
        tile_of = jnp.full((1, table.shape[2]), send_ref[0, group], jnp.int32)
        table[z, group : group + 1, :] = tile_of.astype(jnp.float32)
    for j in range(chunks):
        keep(0, j, block_ref[:, j * width : (j + 1) * width])

    def clear(slot, carry):
        sums[slot] = jnp.zeros(sums.shape[1:], jnp.float32)
        return carry

    def add_slot(slot, carry):
        sums[slot] = sums[before_ref[slot]] + values_ref[slot].astype(jnp.float32)
        return carry

    lax.fori_loop(0, slots + 1, clear, 0)
    load.wait()
    lax.fori_loop(0, slots, add_slot, 0)
    scales = []
    for row in range(row_tiles):
        degree = degree_ref[row : row + 1, :].astype(jnp.float32)
        scales.append((1.0 / jnp.broadcast_to(degree, (tile, tile))).T)

    def part_of(row, col):
        return (sums[last_ref[row * (local + groups) + col]] * scales[row]).astype(jnp.bfloat16)

    for lane in range(lanes):
        for place in range(LINE):
            for row in range(row_tiles):
                across[lane, row * tile : (row + 1) * tile, place * tile : (place + 1) * tile] = part_of(
                    row, local + place * lanes + lane)

    pl.semaphore_wait(barrier, groups + ranks - 2)
    table_copy(far).start()
    for j in range(min(AHEAD, chunks)):
        up_copy(0, j).start()

    @pl.when(inner == 0)
    def _():
        table_copy(hub).start()
        for step in range(lanes):
            give_copy(1, step).start()
        for j in range(min(AHEAD, chunks), chunks):
            up_copy(0, j).start()

    @pl.when(inner == 1)
    def _():
        for step in range(1, lanes):
            give_copy(0, step).start()

    for j in range(chunks):
        row_start(0, j)
    for row in range(row_tiles):
        for col in range(local):
            near[row * tile : (row + 1) * tile, col * tile : (col + 1) * tile] = part_of(row, col)

    def finish(phase, j, in_line):
        row_wait(phase, j)
        summed = jnp.dot(
            near[...], source[phase, j].reshape(-1, width), preferred_element_type=jnp.float32)
        if in_line:
            summed += held[j]
        for step in range(1, lanes) if in_line else range(1 if joined(j) else lanes):
            remote(
                incoming.at[phase, j, step], incoming.at[phase, j, step], part_send.at[phase, j, 0, step],
                part_recv.at[phase, j, step], at(hub, y)).wait_recv()
            summed += incoming[phase, j, step].astype(jnp.float32)
        current = summed.astype(jnp.bfloat16)
        if phase == 0:
            total[j] = current.astype(jnp.float32)
        else:
            total[j] += current.astype(jnp.float32)
        if phase < POWERS - 1:
            keep(phase + 1, j, current)
            up_copy(phase + 1, j).start()
        else:
            logs = jnp.log(jnp.maximum(3.0 * total[j], 1.0)).astype(jnp.bfloat16)
            logs_ref[:, j * width : (j + 1) * width] = logs
            keep(phase + 1, j, logs)
        row_start(phase + 1, j)

    def relay(phase, j):
        line_arrival(phase, j, end).wait_recv()
        relay_copy(phase, j).start()

    def widen(side, step):
        target = (end if side else hub) * lanes + lane_after(step)
        for place in range(LINE):
            row = table[place, pl.ds(target, 1), :]
            piece = given[side, step, :, place * tile : (place + 1) * tile]
            for kind in range(row_tiles):
                chosen = jnp.where(row == float(kind), 1.0, 0.0).astype(jnp.bfloat16)
                spot = (place * row_tiles + kind) * tile
                spread[side, step, :, spot : spot + tile] = piece * chosen

    def partial(phase, j, sides):
        if sides[0] == 0:
            line_arrival(phase, j, far).wait_recv()
            line_arrival(phase, j, far_end).wait_recv()
        matrix = spread[sides[0] : sides[-1] + 1].reshape(-1, spread.shape[-1])
        summed = jnp.dot(matrix, line[phase, j].reshape(-1, width), preferred_element_type=jnp.float32)
        for side in sides:
            for step in reversed(range(lanes)):
                spot = ((side - sides[0]) * lanes + step) * rows_here
                here = summed[spot : spot + rows_here]
                if side == 0 and step == 0:
                    held[j] = here
                elif step == 0 and joined(j):
                    mixed[j // 2] = here
                else:
                    if phase > 0:
                        part_copy(phase - 1, j, side, step).wait_send()
                    outgoing[j, side, step] = here.astype(jnp.bfloat16)
                    part_copy(phase, j, side, step).start()

    def join(phase, j):
        if joined(j):
            summed = mixed[j // 2]
            for step in range(1, lanes):
                spot = joint.at[phase, j // 2, step]
                remote(
                    spot, spot, part_send.at[phase, j, 1, step], joint_recv.at[phase, j // 2, step],
                    at(hub, y)).wait_recv()
                summed += joint[phase, j // 2, step].astype(jnp.float32)
            if phase > 0:
                part_copy(phase - 1, j, 1, 0).wait_send()
            outgoing[j, 1, 0] = summed.astype(jnp.bfloat16)
            part_copy(phase, j, 1, 0).start()

    def take(side):
        for step in range(1 - side, lanes):
            remote(
                given.at[side, step], given.at[side, step], give_send.at[step], give_recv.at[side, step],
                at(hub, y)).wait_recv()
        for step in range(lanes):
            widen(side, step)

    @pl.when(inner == 1)
    def _():
        given[0, 0] = across[y]
        first = min(AHEAD, chunks)
        for j in range(first):
            relay(0, j)
        for j in range(first, chunks):
            up_copy(0, j).start()
        for j in range(first):
            row_pass(0, j)
        for place in (far, end, far_end):
            table_arrival(place).wait_recv()
        take(0)
        for j in range(first):
            partial(0, j, (0,))
        for j in range(first):
            finish(0, j, True)
        take(1)
        for j in range(first):
            partial(0, j, (1,))
        for j in range(first, chunks):
            row_pass(0, j)
        steps = POWERS * chunks
        for n in range(first, min(first + 2, steps)):
            relay(n // chunks, n % chunks)
        for n in range(first, steps + LAG_PASS):
            if n < steps:
                partial(n // chunks, n % chunks, (0, 1))
            m = n - LAG_JOIN
            if 0 <= m < steps:
                join(m // chunks, m % chunks)
            m = n - LAG_FINISH
            if first <= m < steps:
                finish(m // chunks, m % chunks, True)
            for m in relays_after(n, first, chunks, steps):
                relay(m // chunks, m % chunks)
            m = n - LAG_PASS
            if 0 <= m < steps:
                row_pass(m // chunks + 1, m % chunks)
        for phase in range(POWERS):
            for j in range(chunks):
                relay_copy(phase, j).wait_send()
        for j in range(chunks):
            for side in (0, 1):
                for step in range(1 - side, lanes):
                    part_copy(POWERS - 1, j, side, step).wait_send()
        for step in range(1, lanes):
            give_copy(0, step).wait_send()

    @pl.when(inner == 0)
    def _():
        for j in range(chunks):
            row_pass(0, j)
        steps = POWERS * chunks
        for n in range(steps + 1):
            if n < steps:
                finish(n // chunks, n % chunks, False)
            if n > 0:
                row_pass((n - 1) // chunks + 1, (n - 1) % chunks)
        for step in range(lanes):
            give_copy(1, step).wait_send()
        table_copy(hub).wait_send()

    table_copy(far).wait_send()
    for j in range(chunks):
        row_wait(POWERS, j)
    each = chunks // ranks
    for k in range(each):
        mine[k * width : (k + 1) * width, :] = everyone[r * each + k].reshape(-1, width).T
    rows_all = rows_here * ranks
    for j in range(chunks):
        part = jnp.dot(mine[...], everyone[j].reshape(-1, width), preferred_element_type=jnp.float32)
        gram_ref[:, j * width : (j + 1) * width] = part / rows_all
    for phase in range(POWERS + 1):
        for j in range(chunks):
            if phase < POWERS:
                up_copy(phase, j).wait_send()
            for step in range(1, pairs):
                row_copy(phase, j, same_core(step)).wait_send()
                pass_copy(phase, j, lax.rem(r + ranks - 2 * step, ranks)).wait_send()
            row_copy(phase, j, partner).wait_send()


def body(block, degree, tile_values, tile_rows, tile_cols, tile_count, send_tiles):
    rows_here, width = block.shape
    tile = tile_values.shape[1]
    row_tiles = rows_here // tile
    ranks = lax.axis_size("row")
    groups = lax.axis_size("grp")
    local = ranks * row_tiles
    lanes = groups // LINE
    sources = local + groups
    smem = pl.BlockSpec(memory_space=pltpu.SMEM)
    vmem = pl.BlockSpec(memory_space=pltpu.VMEM)
    slots = tile_values.shape[0]
    before, last = pl.pallas_call(
        functools.partial(order_kernel, sources),
        out_shape=(
            jax.ShapeDtypeStruct((slots,), jnp.int32),
            jax.ShapeDtypeStruct((row_tiles * sources,), jnp.int32),
        ),
        in_specs=[smem, smem, smem],
        out_specs=(smem, smem),
        name="order",
    )(tile_rows, tile_cols, tile_count)
    share = width // ranks
    chunks = max(ranks, CHUNKS)
    part = width // chunks
    dma = pltpu.SemaphoreType.DMA
    half = jnp.bfloat16
    logs, gram = pl.pallas_call(
        functools.partial(step_kernel, groups, ranks),
        out_shape=(
            jax.ShapeDtypeStruct((rows_here, width), half),
            jax.ShapeDtypeStruct((share, width), jnp.float32),
        ),
        in_specs=[smem, smem, smem, vmem, pl.BlockSpec(memory_space=pl.ANY), vmem],
        out_specs=(vmem, vmem),
        scratch_shapes=[
            pltpu.VMEM(tile_values.shape, half),
            dma,
            pltpu.VMEM((slots + 1, tile, tile), jnp.float32),
            pltpu.VMEM((rows_here, local * tile), half),
            pltpu.VMEM((lanes, rows_here, LINE * tile), half),
            pltpu.VMEM((LINE, groups, tile), jnp.float32),
            pltpu.VMEM((2, lanes, rows_here, LINE * tile), half),
            pltpu.VMEM((2, lanes, rows_here, LINE * row_tiles * tile), half),
            pltpu.VMEM((POWERS, chunks, local, tile, part), half),
            pltpu.VMEM((POWERS, chunks, LINE, row_tiles, tile, part), half),
            pltpu.VMEM((chunks, 2, lanes, rows_here, part), half),
            pltpu.VMEM((POWERS, chunks, lanes, rows_here, part), half),
            pltpu.VMEM((POWERS, chunks // 2, lanes, rows_here, part), half),
            pltpu.VMEM((chunks, rows_here, part), jnp.float32),
            pltpu.VMEM((chunks // 2, rows_here, part), jnp.float32),
            pltpu.VMEM((chunks, rows_here, part), jnp.float32),
            pltpu.VMEM((chunks, local, tile, part), half),
            pltpu.VMEM((share, rows_here * ranks), half),
            dma((POWERS + 1, chunks, ranks)),
            dma((POWERS + 1, chunks, ranks)),
            dma((POWERS + 1, chunks, ranks)),
            dma((POWERS, chunks)),
            dma((POWERS, chunks)),
            dma((POWERS, chunks, LINE)),
            dma((POWERS, chunks, 2, lanes)),
            dma((POWERS, chunks, lanes)),
            dma((POWERS, chunks // 2, lanes)),
            dma((lanes,)),
            dma((2, lanes)),
            dma((LINE,)),
            dma((LINE,)),
        ],
        compiler_params=pltpu.CompilerParams(
            collective_id=0, has_side_effects=True, vmem_limit_bytes=67043328),
        name="step",
    )(send_tiles, before, last, degree.reshape(row_tiles, tile), tile_values, block)
    return logs, gram


def solution(mesh):
    placed = (
        P(("grp", "row"), None),
        P(("grp", "row")),
        P(("grp", "row"), None, None),
        P(("grp", "row")),
        P(("grp", "row")),
        P(("grp", "row")),
        P(("grp", "row"), None),
    )
    return jax.shard_map(
        body,
        mesh=mesh,
        in_specs=placed,
        out_specs=(P(("grp", "row"), None), P(("grp", "row"), None)),
        check_vma=False,
    )
```

time: 115 us -> 91.8 us (0.80)
  Pallas kernels: 109 us -> 84.8 us
    pallas_call x1, Pallas kernels: 106 us -> 82.6 us  [body(): pl.pallas_call(functools.partial(step_kernel, groups, ranks), out_shape=(...]
where the time goes in v1:
time: 91.8 us; the launch traced here: 90.3 us
  Pallas kernels  84.8 us (92%)
  local copies, waits for them, and re-layouts  4.17 us (5%)
  between operations  1.29 us (1%)
    pallas_call x1, Pallas kernels, body(): pl.pallas_call(functools.partial(step_kernel, groups, ranks), out_shape=(...  82.6 us
    unnamed x2, local copies, waits for them, and re-layouts  4.17 us
    pallas_call x1, Pallas kernels, body(): pl.pallas_call(functools.partial(order_kernel, sources), out_shape=(jax.S...  2.23 us

profile of v1, /device:TPU:1, one launch (start us, length us, event | category | flops | bytes accessed | tf_op | source)
XLA Modules:
  0.0 90.3 jit_solution(18010294706673049940)
XLA Ops:
  1.3 2.2 %order.1 = (s32[64]{0:T(128)}, s32[32]{0:T(128)}) custom-call(s32[64]{0:T(128)} %rows_ref.1, s32[64]{0:T(128)} %cols_ref.1, s32[1]{0:T(128)S(6)} %copy.11.count_ref), custom_call_target="tpu_custom_call" | custom-call | tf_op jit(solution)/shard_map/order/pallas_call | solution.py:408
  3.5 82.6 %step.1 = (bf16[256,1024]{1,0:T(8,128)(2,1)}, f32[256,1024]{1,0:T(8,128)}) custom-call(s32[1,8]{1,0:T(1,128)} %send_ref.1, s32[64]{0:T(128)} %get-tuple-element.4.before_ref, s32[32]{0:T(128)} %get-tuple-element.5.last_ref, s32[2,128]{1,0:T(2,128)} %bitcast.1, bf16[64,128,128]{2,1,0:T(8,128)(2,1)} %values_hbm.1, bf16[256,1024]{1,0:T(8,128)(2,1)} %block_ref.1), custom_call_target="tpu_custom_call" | custom-call | tf_op jit(solution)/shard_map/step/pallas_call | solution.py:423
  86.1 1.9 %copy.12 = bf16[256,1024]{1,0:T(8,128)(2,1)} copy(bf16[256,1024]{1,0:T(8,128)(2,1)} %get-tuple-element.8) | data formatting | bytes 1048576
  88.0 2.3 %copy.13 = f32[256,1024]{1,0:T(8,128)} copy(f32[256,1024]{1,0:T(8,128)} %get-tuple-element.9) | data formatting | bytes 2097152

commit v2 on v1

v2 whole, which is shorter than its diff:
```python
import functools

import jax
import jax.numpy as jnp
from jax import lax
from jax.experimental import pallas as pl
from jax.experimental.pallas import tpu as pltpu
from jax.sharding import PartitionSpec as P

POWERS = 2
LINE = 4
CHUNKS = 8
AHEAD_HUB = 3
AHEAD_END = 4
FORWARD = 3
LAG_FINISH = 2
LAG_RELAY = 4
AHEAD_RELAY = 3
LAG_PASS = 4
LAG_END = 3
MESH = pl.DeviceIdType.MESH


def relays_after(n, first, chunks, steps):
    near = range(min(AHEAD_END, chunks) if first else n + AHEAD_RELAY, n + AHEAD_RELAY + 1)
    later = range(chunks if first else n + LAG_RELAY, n + LAG_RELAY + 1)
    return [m for m in near if m < chunks] + [m for m in later if chunks <= m < steps]


def order_kernel(sources, rows_ref, cols_ref, count_ref, before_ref, last_ref):
    slots = rows_ref.shape[0]

    def clear(place, carry):
        last_ref[place] = slots
        return carry

    def skip(slot, carry):
        before_ref[slot] = slots
        return carry

    def link(slot, carry):
        place = rows_ref[slot] * sources + cols_ref[slot]
        before_ref[slot] = last_ref[place]
        last_ref[place] = slot
        return carry

    lax.fori_loop(0, last_ref.shape[0], clear, 0)
    lax.fori_loop(0, slots, skip, 0)
    lax.fori_loop(0, count_ref[0], link, 0)


def step_kernel(
    groups, ranks, send_ref, before_ref, last_ref, degree_ref, values_hbm, block_ref, gathered_hbm,
    values_sem, sums, near, across, table, given, spread,
    source, arrived, line, outgoing, incoming, everyone,
    row_send, row_recv, pass_send, up_send, relay_send, line_recv, part_send, part_recv,
    give_send, give_recv, table_send, table_recv, side_send, side_recv, tile_send, tile_recv, out_sem,
):
    chunks, local, tile, width = everyone.shape
    early = arrived.shape[0]
    row_tiles = line.shape[3]
    rows_here = row_tiles * tile
    lanes = groups // LINE
    g = lax.axis_index("grp")
    r = lax.axis_index("row")
    z = g // lanes
    y = lax.rem(g, lanes)
    half = z // 2
    inner = lax.rem(z + half, 2)
    hub = 1 + half
    far = 2 - half
    end = 3 * half
    onward = hub + inner * (far - hub)
    core = lax.rem(r, 2)
    partner = r + 1 - 2 * core
    pairs = ranks // 2

    slots = values_hbm.shape[0]
    load = pltpu.make_async_copy(values_hbm, outgoing.at[pl.ds(0, slots)], values_sem)
    load.start()

    def at(place, lane):
        return (place * lanes + lane, r)

    def lane_after(step):
        return lax.rem(y + step, lanes)

    def lane_before(step):
        return lax.rem(y + lanes - step, lanes)

    def same_core(step):
        return lax.rem(r + 2 * step, ranks)

    barrier = pltpu.get_barrier_semaphore()
    for step in range(1, groups):
        pl.semaphore_signal(barrier, inc=1, device_id=(lax.rem(g + step, groups), r), device_id_type=MESH)
    for step in range(1, ranks):
        pl.semaphore_signal(barrier, inc=1, device_id=(g, lax.rem(r + step, ranks)), device_id_type=MESH)

    def remote(src, dst, send_sem, recv_sem, to):
        return pltpu.make_async_remote_copy(
            src_ref=src, dst_ref=dst, send_sem=send_sem, recv_sem=recv_sem, device_id=to, device_id_type=MESH)

    def land(phase, j, rank):
        where = pl.ds(rank * row_tiles, row_tiles)
        return source.at[phase, j, where] if phase < POWERS else everyone.at[j, where]

    def span(phase, rank):
        where = pl.ds(rank * row_tiles, row_tiles)
        return source.at[phase, :, where] if phase < POWERS else everyone.at[:, where]

    def row_copy(phase, j, step):
        spot = land(phase, j, r)
        to = same_core(step) if step else partner
        arrival = step - 1 if step else pairs - 1
        return remote(spot, spot, row_send.at[phase, step], row_recv.at[phase, j, arrival], (g, to))

    def pass_copy(phase, j, step):
        spot = land(phase, j, lax.rem(r + ranks - 2 * step, ranks))
        return remote(
            spot, spot, pass_send.at[phase, step - 1], row_recv.at[phase, j, pairs - 1], (g, partner))

    def up_copy(phase, j):
        return remote(
            land(phase, j, r), line.at[phase, j, 2 * inner], up_send.at[phase], line_recv.at[phase, j, inner],
            at(onward, y))

    def relay_copy(phase, j):
        return remote(
            line.at[phase, j, 0], line.at[phase, j, 3], relay_send.at[phase], line_recv.at[phase, j, 1],
            at(far, y))

    def line_wait(phase, j, where, kind):
        spot = line.at[phase, j, where]
        remote(spot, spot, relay_send.at[phase], line_recv.at[phase, j, kind], at(far, y)).wait_recv()

    def out_spot(j, side, step):
        return ((j * 2 + side) * lanes + step) * row_tiles

    def side_copy(phase, j, step):
        return remote(
            outgoing.at[out_spot(j, phase, step)], source.at[phase, j, local + step], side_send.at[phase, step],
            side_recv.at[phase, j], at(end, lane_after(step)))

    def tile_copy(j, step, own):
        where = pl.ds(0, 1) if own else pl.ds(1, LINE - 2)
        return remote(
            arrived.at[j, step, where], arrived.at[j, step, where], tile_send.at[1 - own], tile_recv.at[j],
            at(end, lane_after(step)))

    def part_copy(phase, j, side, step):
        return remote(
            outgoing.at[pl.ds(out_spot(j, side, step), row_tiles)], incoming.at[phase, j, step],
            part_send.at[j, side, step], part_recv.at[phase, j],
            at(end if side else hub, lane_after(step)))

    def give_copy(side, step):
        return remote(
            across.at[lane_before(step), side:], given.at[side, step, side:],
            give_send.at[step], give_recv.at[side, step], at(hub, lane_before(step)))

    def table_copy(to, place, sem):
        return remote(table.at[inner], table.at[place], table_send.at[sem], table_recv.at[0], at(to, y))

    def keep(phase, j, value):
        tiles = value.reshape(row_tiles, tile, width)
        if phase < POWERS:
            source[phase, j, pl.ds(r * row_tiles, row_tiles)] = tiles
            line[phase, j, 1] = tiles
        else:
            everyone[j, pl.ds(r * row_tiles, row_tiles)] = tiles

    def wanted(phase, j, group):
        picked = source[phase, j, r * row_tiles]
        for kind in range(1, row_tiles):
            picked = jnp.where(send_ref[0, group] == kind, source[phase, j, r * row_tiles + kind], picked)
        return picked

    def beside(phase, j):
        for step in range(1, lanes):
            outgoing[out_spot(j, phase, step)] = wanted(phase, j, end * lanes + lane_after(step))
            side_copy(phase, j, step).start()
        source[phase, j, local] = wanted(phase, j, g)

    def forward_own(j):
        for step in range(lanes):
            arrived[j, step, 0] = wanted(0, j, end * lanes + lane_after(step))
            tile_copy(j, step, 1).start()

    def forward_rest(j):
        line_wait(0, j, pl.ds(2, 2), 1)
        for step in range(lanes):
            for place in range(2, LINE):
                row = table[place, pl.ds(end * lanes + lane_after(step), 1), :]
                picked = line[0, j, place, 0]
                for kind in range(1, row_tiles):
                    chosen = jnp.where(row == float(kind), 1.0, 0.0).astype(jnp.bfloat16)
                    picked = picked * (1 - chosen) + line[0, j, place, kind] * chosen
                arrived[j, step, place - 1] = picked
            tile_copy(j, step, 0).start()

    def row_start(phase, j):
        for step in (*range(1, pairs), 0):
            row_copy(phase, j, step).start()

    def row_pass(phase, j):
        for step in range(1, pairs):
            rank = lax.rem(r + ranks - 2 * step, ranks)
            spot = land(phase, j, rank)
            remote(spot, spot, row_send.at[phase, 0], row_recv.at[phase, j, step - 1], (g, partner)).wait_recv()
            pass_copy(phase, j, step).start()

    def row_wait(phase, j):
        where = pl.ds(0, pairs * row_tiles)
        spot = source.at[phase, j, where] if phase < POWERS else everyone.at[j, where]
        remote(spot, spot, row_send.at[phase, 0], row_recv.at[phase, j, pairs - 1], (g, partner)).wait_recv()

    for group in range(groups):
        tile_of = jnp.full((1, table.shape[2]), send_ref[0, group], jnp.int32)
        table[inner, group : group + 1, :] = tile_of.astype(jnp.float32)
    for j in range(chunks):
        keep(0, j, block_ref[:, j * width : (j + 1) * width])

    def clear(slot, carry):
        sums[slot] = jnp.zeros(sums.shape[1:], jnp.float32)
        return carry

    def add_slot(slot, carry):
        sums[slot] = sums[before_ref[slot]] + outgoing[slot].astype(jnp.float32)
        return carry

    lax.fori_loop(0, slots + 1, clear, 0)
    load.wait()
    lax.fori_loop(0, slots, add_slot, 0)
    scales = []
    for row in range(row_tiles):
        degree = degree_ref[row : row + 1, :].astype(jnp.float32)
        scales.append((1.0 / jnp.broadcast_to(degree, (tile, tile))).T)

    def part_of(row, col):
        return (sums[last_ref[row * (local + groups) + col]] * scales[row]).astype(jnp.bfloat16)

    for lane in range(lanes):
        for place in range(LINE):
            rank = place + half * (LINE - 1 - 2 * place)
            for row in range(row_tiles):
                across[lane, rank, row * tile : (row + 1) * tile, :] = part_of(row, local + place * lanes + lane)

    pl.semaphore_wait(barrier, groups + ranks - 2)
    table_copy(far, 3 - inner, 0).start()

    @pl.when(inner == 0)
    def _():
        for j in range(min(AHEAD_END, chunks)):
            up_copy(0, j).start()
        table_copy(hub, 0, 1).start()
        for step in range(lanes):
            give_copy(1, step).start()
        for j in range(min(AHEAD_END, chunks), chunks):
            up_copy(0, j).start()

    @pl.when(inner == 1)
    def _():
        for j in range(min(AHEAD_HUB, chunks)):
            up_copy(0, j).start()
        for step in range(1, lanes):
            give_copy(0, step).start()
        for j in range(early):
            forward_own(j)

    for j in range(chunks):
        row_start(0, j)

    @pl.when(inner == 0)
    def _():
        for j in range(chunks):
            beside(0, j)

    for row in range(row_tiles):
        for col in range(local):
            near[row * tile : (row + 1) * tile, col * tile : (col + 1) * tile] = part_of(row, col)
    def finish(phase, j, in_line):
        row_wait(phase, j)
        if in_line:
            kept = sums[pl.ds(j * row_tiles, row_tiles)].reshape(rows_here, width)
            summed = kept + jnp.dot(
                near[...], source[phase, j, :local].reshape(-1, width),
                preferred_element_type=jnp.float32)
        else:
            spot = source.at[phase, j, pl.ds(local + 1, lanes - 1)]
            remote(spot, spot, side_send.at[phase, 0], side_recv.at[phase, j], at(end, y)).wait_recv()
            matrix = jnp.concatenate(
                [near[...]] + [across[lane_before(step), 0] for step in range(lanes)], axis=1)
            summed = jnp.dot(
                matrix, source[phase, j].reshape(-1, width), preferred_element_type=jnp.float32)
        direct = phase == 0 and j < early and not in_line
        if direct:
            spot = arrived.at[j]
            remote(spot, spot, tile_send.at[0], tile_recv.at[j], at(end, y)).wait_recv()
            matrix = jnp.concatenate(
                [across[lane_before(step), place] for step in range(lanes) for place in range(1, LINE)], axis=1)
            summed += jnp.dot(matrix, arrived[j].reshape(-1, width), preferred_element_type=jnp.float32)
        first = lanes if direct else 1 if in_line else 0
        if first < lanes:
            spot = incoming.at[phase, j, pl.ds(first, lanes - first)]
            remote(spot, spot, part_send.at[j, 0, 0], part_recv.at[phase, j], at(hub, y)).wait_recv()
        for step in range(first, lanes):
            summed += incoming[phase, j, step].reshape(rows_here, width).astype(jnp.float32)
        current = summed.astype(jnp.bfloat16)
        if phase < POWERS - 1:
            keep(phase + 1, j, current)
            up_copy(phase + 1, j).start()
            if not in_line:
                beside(phase + 1, j)
        else:
            power_sum = current.astype(jnp.float32)
            for past in range(1, POWERS):
                mine = source[past, j, pl.ds(r * row_tiles, row_tiles)].reshape(rows_here, width)
                power_sum = mine.astype(jnp.float32) + power_sum
            keep(phase + 1, j, jnp.log(jnp.maximum(3.0 * power_sum, 1.0)).astype(jnp.bfloat16))
        row_start(phase + 1, j)

    def relay(phase, j):
        line_wait(phase, j, 0, 0)
        relay_copy(phase, j).start()

    def widen(side, step):
        target = (end if side else hub) * lanes + lane_after(step)
        for place in range(side, LINE):
            row = table[place, pl.ds(target, 1), :]
            piece = given[side, step, place]
            for kind in range(row_tiles):
                chosen = jnp.where(row == float(kind), 1.0, 0.0).astype(jnp.bfloat16)
                spot = (place * row_tiles + kind) * tile
                spread[side, step, :, spot : spot + tile] = piece * chosen

    def partial(phase, j, sides):
        if phase > 0 or j >= early:
            line_wait(phase, j, pl.ds(2, 2), 1)
        for side in sides:
            matrix = spread[side, :, :, side * row_tiles * tile :].reshape(lanes * rows_here, -1)
            summed = jnp.dot(
                matrix, line[phase, j, side:].reshape(-1, width), preferred_element_type=jnp.float32)
            for step in reversed(range(lanes)):
                here = summed[step * rows_here : (step + 1) * rows_here]
                if side == 0 and step == 0:
                    sums[pl.ds(j * row_tiles, row_tiles)] = here.reshape(row_tiles, tile, width)
                else:
                    if phase > 1 or (phase == 1 and (side == 0 or j >= early)):
                        part_copy(phase - 1, j, side, step).wait_send()
                    where = pl.ds(out_spot(j, side, step), row_tiles)
                    outgoing[where] = here.astype(jnp.bfloat16).reshape(row_tiles, tile, width)
                    part_copy(phase, j, side, step).start()

    def take(side):
        for step in range(1 - side, lanes):
            spot = given.at[side, step, side:]
            remote(spot, spot, give_send.at[step], give_recv.at[side, step], at(hub, y)).wait_recv()
        for step in range(lanes):
            widen(side, step)

    @pl.when(inner == 1)
    def _():
        given[0, 0] = across[y]
        sent = min(AHEAD_HUB, chunks)
        for j in range(min(AHEAD_END, chunks)):
            relay(0, j)
            if sent < chunks:
                up_copy(0, sent).start()
                sent += 1
        for j in range(sent, chunks):
            up_copy(0, j).start()
        spot = table.at[pl.ds(0, LINE - 1)]
        remote(spot, spot, table_send.at[0], table_recv.at[0], at(far, y)).wait_recv()
        for j in range(early):
            row_pass(0, j)
        for j in range(early):
            forward_rest(j)
            if j == 0:
                take(0)
            partial(0, j, (0,))
            if j > 0:
                finish(0, j - 1, True)
        for j in range(early, chunks):
            row_pass(0, j)
        take(1)
        steps = POWERS * chunks
        for n in range(early, steps + LAG_PASS):
            if n < steps:
                partial(n // chunks, n % chunks, (0, 1))
            m = n - LAG_FINISH
            if early - 1 <= m < steps:
                finish(m // chunks, m % chunks, True)
            for m in relays_after(n, n == early, chunks, steps):
                relay(m // chunks, m % chunks)
            m = n - LAG_PASS
            if 0 <= m < steps:
                row_pass(m // chunks + 1, m % chunks)
        for own in (0, 1):
            spot = arrived.at[:, :, pl.ds(0, 1) if own else pl.ds(1, LINE - 2)]
            remote(spot, spot, tile_send.at[1 - own], tile_recv.at[0], at(end, y)).wait_send()
        for phase in range(POWERS):
            spot = line.at[phase, :, 0]
            remote(spot, spot, relay_send.at[phase], line_recv.at[phase, 0, 0], at(far, y)).wait_send()
        for j in range(chunks):
            for side in (0, 1):
                for step in range(1 - side, lanes):
                    part_copy(POWERS - 1, j, side, step).wait_send()
        for step in range(1, lanes):
            give_copy(0, step).wait_send()

    @pl.when(inner == 0)
    def _():
        steps = POWERS * chunks
        for j in range(min(AHEAD_END, chunks)):
            row_pass(0, j)
        for n in range(steps + LAG_END):
            if n < steps:
                finish(n // chunks, n % chunks, False)
            if min(AHEAD_END, chunks) + n < chunks:
                row_pass(0, min(AHEAD_END, chunks) + n)
            m = n - LAG_END
            if m >= 0:
                row_pass(m // chunks + 1, m % chunks)
        for step in range(lanes):
            give_copy(1, step).wait_send()
        for phase in range(POWERS):
            for step in range(1, lanes):
                spot = outgoing.at[pl.ds(0, chunks)]
                remote(spot, spot, side_send.at[phase, step], side_recv.at[phase, 0], at(end, y)).wait_send()
        table_copy(hub, 0, 1).wait_send()

    def row_sent(phase):
        for step in range(pairs):
            spot = span(phase, r)
            remote(spot, spot, row_send.at[phase, step], row_recv.at[phase, 0, 0], (g, partner)).wait_send()
        for step in range(1, pairs):
            spot = span(phase, lax.rem(r + ranks - 2 * step, ranks))
            remote(spot, spot, pass_send.at[phase, step - 1], row_recv.at[phase, 0, 0], (g, partner)).wait_send()

    table_copy(far, 3 - inner, 0).wait_send()
    for phase in range(POWERS):
        spot = span(phase, r)
        remote(spot, spot, up_send.at[phase], line_recv.at[phase, 0, 0], at(onward, y)).wait_send()
        row_sent(phase)
    for j in range(chunks):
        row_wait(POWERS, j)
        pltpu.make_async_copy(everyone.at[j], gathered_hbm.at[j], out_sem.at[0]).start()
    row_sent(POWERS)
    pltpu.make_async_copy(everyone, gathered_hbm, out_sem.at[0]).wait()


def gram_kernel(ranks, gathered_hbm, logs_hbm, gram_hbm, gathered, mine, logs, gram, in_sem, logs_sem, out_sem):
    chunks, local, tile, width = gathered.shape
    rows_here = local // ranks * tile
    r = lax.axis_index("row")
    each = chunks // ranks

    def in_copy(j):
        return pltpu.make_async_copy(gathered_hbm.at[j], gathered.at[j], in_sem.at[j])

    def out_copy(k):
        where = pl.ds(pl.multiple_of(k * each * width, width), each * width)
        return pltpu.make_async_copy(gram.at[:, where], gram_hbm.at[:, where], out_sem.at[k])

    def logs_copy(k):
        where = pl.ds(pl.multiple_of(k * each * width, width), each * width)
        return pltpu.make_async_copy(logs.at[:, where], logs_hbm.at[:, where], logs_sem.at[k])

    for j in range(chunks):
        in_copy(lax.rem(r * each + j, chunks)).start()
    for j in range(each):
        in_copy(r * each + j).wait()
        mine[j * width : (j + 1) * width, :] = gathered[r * each + j].reshape(-1, width).T
    own = pl.ds(r * (local // ranks), local // ranks)
    for step in range(ranks):
        k = lax.rem(r + step, ranks)
        if step:
            for j in range(each):
                in_copy(k * each + j).wait()
        block = jnp.concatenate([gathered[k * each + j].reshape(-1, width) for j in range(each)], axis=1)
        part = jnp.dot(mine[...], block, preferred_element_type=jnp.float32) / (rows_here * ranks)
        where = pl.ds(pl.multiple_of(k * each * width, width), each * width)
        gram[:, where] = part
        out_copy(k).start()
        logs[:, where] = jnp.concatenate(
            [gathered[k * each + j, own].reshape(rows_here, width) for j in range(each)], axis=1)
        logs_copy(k).start()
    for k in range(ranks):
        out_copy(k).wait()
        logs_copy(k).wait()


def body(block, degree, tile_values, tile_rows, tile_cols, tile_count, send_tiles):
    rows_here, width = block.shape
    tile = tile_values.shape[1]
    row_tiles = rows_here // tile
    ranks = lax.axis_size("row")
    groups = lax.axis_size("grp")
    local = ranks * row_tiles
    lanes = groups // LINE
    sources = local + groups
    smem = pl.BlockSpec(memory_space=pltpu.SMEM)
    vmem = pl.BlockSpec(memory_space=pltpu.VMEM)
    slots = tile_values.shape[0]
    before, last = pl.pallas_call(
        functools.partial(order_kernel, sources),
        out_shape=(
            jax.ShapeDtypeStruct((slots,), jnp.int32),
            jax.ShapeDtypeStruct((row_tiles * sources,), jnp.int32),
        ),
        in_specs=[smem, smem, smem],
        out_specs=(smem, smem),
        name="order",
    )(tile_rows, tile_cols, tile_count)
    share = width // ranks
    early = max(1, min(FORWARD, 8 // lanes))
    pairs = ranks // 2
    chunks = max(ranks, CHUNKS)
    part = width // chunks
    dma = pltpu.SemaphoreType.DMA
    half = jnp.bfloat16
    anywhere = pl.BlockSpec(memory_space=pl.ANY)
    gathered = pl.pallas_call(
        functools.partial(step_kernel, groups, ranks),
        out_shape=jax.ShapeDtypeStruct((chunks, local, tile, part), half),
        in_specs=[smem, smem, smem, vmem, anywhere, vmem],
        out_specs=anywhere,
        scratch_shapes=[
            dma,
            pltpu.VMEM((slots + 1, tile, tile), jnp.float32),
            pltpu.VMEM((rows_here, local * tile), half),
            pltpu.VMEM((lanes, LINE, rows_here, tile), half),
            pltpu.VMEM((LINE, groups, tile), jnp.float32),
            pltpu.VMEM((2, lanes, LINE, rows_here, tile), half),
            pltpu.VMEM((2, lanes, rows_here, LINE * row_tiles * tile), half),
            pltpu.VMEM((POWERS, chunks, local + lanes, tile, part), half),
            pltpu.VMEM((early, lanes, LINE - 1, tile, part), half),
            pltpu.VMEM((POWERS, chunks, LINE, row_tiles, tile, part), half),
            pltpu.VMEM((chunks * 2 * lanes * row_tiles, tile, part), half),
            pltpu.VMEM((POWERS, chunks, lanes, row_tiles, tile, part), half),
            pltpu.VMEM((chunks, local, tile, part), half),
            dma((POWERS + 1, pairs)),
            dma((POWERS + 1, chunks, pairs)),
            dma((POWERS + 1, pairs)),
            dma((POWERS,)),
            dma((POWERS,)),
            dma((POWERS, chunks, 2)),
            dma((chunks, 2, lanes)),
            dma((POWERS, chunks)),
            dma((lanes,)),
            dma((2, lanes)),
            dma((2,)),
            dma((1,)),
            dma((POWERS, lanes)),
            dma((POWERS, chunks)),
            dma((2,)),
            dma((early,)),
            dma((1,)),
        ],
        compiler_params=pltpu.CompilerParams(
            collective_id=0, has_side_effects=True, vmem_limit_bytes=67043328),
        name="step",
    )(send_tiles, before, last, degree.reshape(row_tiles, tile), tile_values, block)
    return tuple(pl.pallas_call(
        functools.partial(gram_kernel, ranks),
        out_shape=(
            jax.ShapeDtypeStruct((rows_here, width), half),
            jax.ShapeDtypeStruct((share, width), jnp.float32),
        ),
        in_specs=[anywhere],
        out_specs=(anywhere, anywhere),
        scratch_shapes=[
            pltpu.VMEM(gathered.shape, half),
            pltpu.VMEM((share, rows_here * ranks), half),
            pltpu.VMEM((rows_here, width), half),
            pltpu.VMEM((share, width), jnp.float32),
            dma((chunks,)),
            dma((ranks,)),
            dma((ranks,)),
        ],
        name="gram",
    )(gathered))


def solution(mesh):
    placed = (
        P(("grp", "row"), None),
        P(("grp", "row")),
        P(("grp", "row"), None, None),
        P(("grp", "row")),
        P(("grp", "row")),
        P(("grp", "row")),
        P(("grp", "row"), None),
    )
    return jax.shard_map(
        body,
        mesh=mesh,
        in_specs=placed,
        out_specs=(P(("grp", "row"), None), P(("grp", "row"), None)),
        check_vma=False,
    )
```

time: 91.8 us -> 80.1 us (0.87); the launches traced: 90.3 us -> 80.2 us
  Pallas kernels: 84.8 us -> 78.7 us
  local copies, waits for them, and re-layouts: 4.17 us -> 0 us
    pallas_call x1 -> x2, Pallas kernels: 82.6 us -> 76.7 us  [the longest x1 73.1 us: body(): pl.pallas_call(functools.partial(step_kernel, groups, ranks), out_shape=j...]
    unnamed x2 -> x0, local copies, waits for them, and re-layouts: 4.17 us -> none
where the time goes in v2:
time: 80.1 us; the launch traced here: 80.2 us
  Pallas kernels  78.7 us (98%)
  between operations  1.47 us (2%)
    pallas_call x1, Pallas kernels, body(): pl.pallas_call(functools.partial(step_kernel, groups, ranks), out_shape=j...  73.1 us
    pallas_call x1, Pallas kernels, body(): pl.pallas_call(functools.partial(gram_kernel, ranks), out_shape=(jax.Shap...  3.63 us
    pallas_call x1, Pallas kernels, body(): pl.pallas_call(functools.partial(order_kernel, sources), out_shape=(jax.S...  2.06 us

profile of v2, /device:TPU:1, one launch (start us, length us, event | category | flops | bytes accessed | tf_op | source)
XLA Modules:
  0.0 80.2 jit_solution(14674090662922535395)
XLA Ops:
  1.3 2.1 %order.1 = (s32[64]{0:T(128)}, s32[32]{0:T(128)}) custom-call(s32[64]{0:T(128)} %rows_ref.1, s32[64]{0:T(128)} %cols_ref.1, s32[1]{0:T(128)S(6)} %copy.9.count_ref), custom_call_target="tpu_custom_call" | custom-call | tf_op jit(solution)/shard_map/order/pallas_call | solution.py:506
  3.3 73.1 %step.1.gathered_hbm = bf16[8,8,128,128]{3,2,1,0:T(8,128)(2,1)} custom-call(s32[1,8]{1,0:T(1,128)} %send_ref.1, s32[64]{0:T(128)} %get-tuple-element.4.before_ref, s32[32]{0:T(128)} %get-tuple-element.5.last_ref, s32[2,128]{1,0:T(2,128)} %bitcast.1, bf16[64,128,128]{2,1,0:T(8,128)(2,1)} %values_hbm.1, bf16[256,1024]{1,0:T(8,128)(2,1)} %block_ref.1), custom_call_target="tpu_custom_call" | custom-call | tf_op jit(solution)/shard_map/step/pallas_call | solution.py:524
  76.4 3.6 %gram.1 = (bf16[256,1024]{1,0:T(8,128)(2,1)}, f32[256,1024]{1,0:T(8,128)}) custom-call(bf16[8,8,128,128]{3,2,1,0:T(8,128)(2,1)} %step.1.gathered_hbm), custom_call_target="tpu_custom_call" | custom-call | tf_op jit(solution)/shard_map/gram/pallas_call | solution.py:565

commit v3 on v2

--- a/solution.py
+++ b/solution.py
@@ -13,10 +13,11 @@
 AHEAD_HUB = 3
 AHEAD_END = 4
 FORWARD = 3
-LAG_FINISH = 2
+LAG_JOIN = 2
+LAG_FINISH = 5
 LAG_RELAY = 4
 AHEAD_RELAY = 3
-LAG_PASS = 4
+LAG_PASS = 7
 LAG_END = 3
 MESH = pl.DeviceIdType.MESH
 
@@ -54,7 +55,7 @@
     values_sem, sums, near, across, table, given, spread,
     source, arrived, line, outgoing, incoming, everyone,
     row_send, row_recv, pass_send, up_send, relay_send, line_recv, part_send, part_recv,
-    give_send, give_recv, table_send, table_recv, side_send, side_recv, tile_send, tile_recv, out_sem,
+    give_send, give_recv, table_send, table_recv, side_send, side_recv, tile_send, tile_recv, joint_recv, out_sem,
 ):
     chunks, local, tile, width = everyone.shape
     early = arrived.shape[0]
@@ -148,7 +149,14 @@
             arrived.at[j, step, where], arrived.at[j, step, where], tile_send.at[1 - own], tile_recv.at[j],
             at(end, lane_after(step)))
 
+    def joined(phase, j):
+        return lanes == 2 and phase == POWERS - 1 and j % 2 == 0 and j < chunks - 2
+
     def part_copy(phase, j, side, step):
+        if side and step and joined(phase, j):
+            return remote(
+                outgoing.at[pl.ds(out_spot(j, side, step), row_tiles)], incoming.at[phase, j, 0],
+                part_send.at[j, side, step], joint_recv.at[j], at(hub, lane_after(step)))
         return remote(
             outgoing.at[pl.ds(out_spot(j, side, step), row_tiles)], incoming.at[phase, j, step],
             part_send.at[j, side, step], part_recv.at[phase, j],
@@ -301,10 +309,11 @@
                 [across[lane_before(step), place] for step in range(lanes) for place in range(1, LINE)], axis=1)
             summed += jnp.dot(matrix, arrived[j].reshape(-1, width), preferred_element_type=jnp.float32)
         first = lanes if direct else 1 if in_line else 0
-        if first < lanes:
-            spot = incoming.at[phase, j, pl.ds(first, lanes - first)]
+        last = 1 if joined(phase, j) and not in_line else lanes
+        if first < last:
+            spot = incoming.at[phase, j, pl.ds(first, last - first)]
             remote(spot, spot, part_send.at[j, 0, 0], part_recv.at[phase, j], at(hub, y)).wait_recv()
-        for step in range(first, lanes):
+        for step in range(first, last):
             summed += incoming[phase, j, step].reshape(rows_here, width).astype(jnp.float32)
         current = summed.astype(jnp.bfloat16)
         if phase < POWERS - 1:
@@ -345,12 +354,24 @@
                 here = summed[step * rows_here : (step + 1) * rows_here]
                 if side == 0 and step == 0:
                     sums[pl.ds(j * row_tiles, row_tiles)] = here.reshape(row_tiles, tile, width)
+                elif step == 0 and joined(phase, j):
+                    sums[pl.ds((chunks + j) * row_tiles, row_tiles)] = here.reshape(row_tiles, tile, width)
                 else:
                     if phase > 1 or (phase == 1 and (side == 0 or j >= early)):
                         part_copy(phase - 1, j, side, step).wait_send()
                     where = pl.ds(out_spot(j, side, step), row_tiles)
                     outgoing[where] = here.astype(jnp.bfloat16).reshape(row_tiles, tile, width)
                     part_copy(phase, j, side, step).start()
+
+    def join(phase, j):
+        if joined(phase, j):
+            spot = incoming.at[phase, j, 0]
+            remote(spot, spot, part_send.at[j, 1, 1], joint_recv.at[j], at(hub, y)).wait_recv()
+            summed = sums[pl.ds((chunks + j) * row_tiles, row_tiles)] + incoming[phase, j, 0].astype(jnp.float32)
+            if j >= early:
+                part_copy(phase - 1, j, 1, 0).wait_send()
+            outgoing[pl.ds(out_spot(j, 1, 0), row_tiles)] = summed.astype(jnp.bfloat16)
+            part_copy(phase, j, 1, 0).start()
 
     def take(side):
         for step in range(1 - side, lanes):
@@ -388,6 +409,9 @@
         for n in range(early, steps + LAG_PASS):
             if n < steps:
                 partial(n // chunks, n % chunks, (0, 1))
+            m = n - LAG_JOIN
+            if early <= m < steps:
+                join(m // chunks, m % chunks)
             m = n - LAG_FINISH
             if early - 1 <= m < steps:
                 finish(m // chunks, m % chunks, True)
@@ -556,6 +580,7 @@
             dma((POWERS, chunks)),
             dma((2,)),
             dma((early,)),
+            dma((chunks,)),
             dma((1,)),
         ],
         compiler_params=pltpu.CompilerParams(

time: 80.1 us -> 76 us (0.949)
  Pallas kernels: 78.7 us -> 74.1 us
    pallas_call x1, Pallas kernels: 73.1 us -> 68.4 us  [body(): pl.pallas_call(functools.partial(step_kernel, groups, ranks), out_shape=j...]
where the time goes in v3:
time: 76 us; the launch traced here: 75.6 us
  Pallas kernels  74.1 us (97%)
  between operations  1.47 us (2%)
    pallas_call x1, Pallas kernels, body(): pl.pallas_call(functools.partial(step_kernel, groups, ranks), out_shape=j...  68.4 us
    pallas_call x1, Pallas kernels, body(): pl.pallas_call(functools.partial(gram_kernel, ranks), out_shape=(jax.Shap...  3.63 us
    pallas_call x1, Pallas kernels, body(): pl.pallas_call(functools.partial(order_kernel, sources), out_shape=(jax.S...  2.1 us

profile of v3, /device:TPU:1, one launch (start us, length us, event | category | flops | bytes accessed | tf_op | source)
XLA Modules:
  0.0 75.6 jit_solution(18024920587544612453)
XLA Ops:
  1.3 2.1 %order.1 = (s32[64]{0:T(128)}, s32[32]{0:T(128)}) custom-call(s32[64]{0:T(128)} %rows_ref.1, s32[64]{0:T(128)} %cols_ref.1, s32[1]{0:T(128)S(6)} %copy.9.count_ref), custom_call_target="tpu_custom_call" | custom-call | tf_op jit(solution)/shard_map/order/pallas_call | solution.py:530
  3.4 68.4 %step.1.gathered_hbm = bf16[8,8,128,128]{3,2,1,0:T(8,128)(2,1)} custom-call(s32[1,8]{1,0:T(1,128)} %send_ref.1, s32[64]{0:T(128)} %get-tuple-element.4.before_ref, s32[32]{0:T(128)} %get-tuple-element.5.last_ref, s32[2,128]{1,0:T(2,128)} %bitcast.1, bf16[64,128,128]{2,1,0:T(8,128)(2,1)} %values_hbm.1, bf16[256,1024]{1,0:T(8,128)(2,1)} %block_ref.1), custom_call_target="tpu_custom_call" | custom-call | tf_op jit(solution)/shard_map/step/pallas_call | solution.py:548
  71.8 3.6 %gram.1 = (bf16[256,1024]{1,0:T(8,128)(2,1)}, f32[256,1024]{1,0:T(8,128)}) custom-call(bf16[8,8,128,128]{3,2,1,0:T(8,128)(2,1)} %step.1.gathered_hbm), custom_call_target="tpu_custom_call" | custom-call | tf_op jit(solution)/shard_map/gram/pallas_call | solution.py:590

commit v4 on v3

--- a/solution.py
+++ b/solution.py
@@ -14,10 +14,10 @@
 AHEAD_END = 4
 FORWARD = 3
 LAG_JOIN = 2
-LAG_FINISH = 5
+LAG_FINISH = 6
 LAG_RELAY = 4
 AHEAD_RELAY = 3
-LAG_PASS = 7
+LAG_PASS = 8
 LAG_END = 3
 MESH = pl.DeviceIdType.MESH
 

time: 76 us -> 78.3 us (1.030); the launches traced: 75.6 us -> 76.9 us
  Pallas kernels: 74.1 us -> 75.5 us
    pallas_call x1, Pallas kernels: 68.4 us -> 69.7 us  [body(): pl.pallas_call(functools.partial(step_kernel, groups, ranks), out_shape=j...]
where the time goes in v4:
time: 78.3 us; the launch traced here: 76.9 us
  Pallas kernels  75.5 us (96%)
  between operations  1.45 us (2%)
    pallas_call x1, Pallas kernels, body(): pl.pallas_call(functools.partial(step_kernel, groups, ranks), out_shape=j...  69.7 us
    pallas_call x1, Pallas kernels, body(): pl.pallas_call(functools.partial(gram_kernel, ranks), out_shape=(jax.Shap...  3.63 us
    pallas_call x1, Pallas kernels, body(): pl.pallas_call(functools.partial(order_kernel, sources), out_shape=(jax.S...  2.11 us

profile of v4, /device:TPU:1, one launch (start us, length us, event | category | flops | bytes accessed | tf_op | source)
XLA Modules:
  0.0 76.9 jit_solution(6262104720852983686)
XLA Ops:
  1.3 2.1 %order.1 = (s32[64]{0:T(128)}, s32[32]{0:T(128)}) custom-call(s32[64]{0:T(128)} %rows_ref.1, s32[64]{0:T(128)} %cols_ref.1, s32[1]{0:T(128)S(6)} %copy.9.count_ref), custom_call_target="tpu_custom_call" | custom-call | tf_op jit(solution)/shard_map/order/pallas_call | solution.py:530
  3.4 69.7 %step.1.gathered_hbm = bf16[8,8,128,128]{3,2,1,0:T(8,128)(2,1)} custom-call(s32[1,8]{1,0:T(1,128)} %send_ref.1, s32[64]{0:T(128)} %get-tuple-element.4.before_ref, s32[32]{0:T(128)} %get-tuple-element.5.last_ref, s32[2,128]{1,0:T(2,128)} %bitcast.1, bf16[64,128,128]{2,1,0:T(8,128)(2,1)} %values_hbm.1, bf16[256,1024]{1,0:T(8,128)(2,1)} %block_ref.1), custom_call_target="tpu_custom_call" | custom-call | tf_op jit(solution)/shard_map/step/pallas_call | solution.py:548
  73.1 3.6 %gram.1 = (bf16[256,1024]{1,0:T(8,128)(2,1)}, f32[256,1024]{1,0:T(8,128)}) custom-call(bf16[8,8,128,128]{3,2,1,0:T(8,128)(2,1)} %step.1.gathered_hbm), custom_call_target="tpu_custom_call" | custom-call | tf_op jit(solution)/shard_map/gram/pallas_call | solution.py:590
